TPU v7x, 128 devices: a whole 4x4x4 slice. The times are simulated.
128 devices in a mesh: quant: 16 (over y, x_lo, core), head: 8 (over x_hi, z).
Axes of the slice: x: 4 (x_hi: 2, x_lo: 2; x = x_hi * 2 + x_lo), y: 4, z: 4, core: 2. Of those that a mesh axis runs over, the one named last changes fastest.
Arguments:
- tokens: bfloat16 [24576, 8192], P('quant', 'head'), may hold values from -6 to 6
- packed_words: int32 [2048, 2048], P('head', 'quant'), may hold values from 0 to 65535
- scales: float32 [64, 2048], replicated, may hold values from 0.0008 to 0.008
- act_order: int32 [8192], replicated, may hold values from 0 to 8191, each once
- head_map: int32 [8], replicated, may hold values from 0 to 7, each once
Outputs:
- keys_out: bfloat16 [24576, 1024], P('quant', 'head')
- values_out: bfloat16 [24576, 1024], P('quant', 'head')
Inputs may be any that keep to these rules, and one draw needn't show every extreme that they name: Bits 4k to 4k + 3 of packed_words[p, c] hold the code of permuted row 4p + k, for k < 4; the other bits are zero. `act_order`: a permutation of the input features. `head_map`: a permutation of the key-value heads.
All inputs are finite; a program needn't handle non-finite values.
Results may differ from a plain program's by a relative error of at most 0.0049.
Values may be sent and summed in bfloat16 or wider, within the bound.
No kernel may reach another device: no remote copies, remote signals or barrier semaphores. Data moves between devices by JAX's collectives and lax.ppermute only.
A program may use at most 128 MiB of HBM per device.

v0:
```python
import functools
import jax
import jax.numpy as jnp
from jax import lax
from jax.experimental import pallas as pl
from jax.experimental.pallas import tpu as pltpu
from jax.sharding import PartitionSpec as P


HD = 128
G = 128
CAP = 192
TILE = 256


def over_head(value, dx, dz):
    pairs = [
        (xh * 4 + z, (xh ^ dx) * 4 + (z + dz) % 4) for xh in range(2) for z in range(4)
    ]
    return lax.ppermute(value, "head", pairs)


def over_quant(value, dy, dx, dc):
    pairs = [
        (y * 4 + x * 2 + c, (y + dy) % 4 * 4 + (x ^ dx) * 2 + (c ^ dc))
        for y in range(4)
        for x in range(2)
        for c in range(2)
    ]
    return lax.ppermute(value, "quant", pairs)


def cost(flops, moved):
    return pl.CostEstimate(flops=flops, bytes_accessed=moved, transcendentals=0)


def vmem(count):
    return [pl.BlockSpec(memory_space=pltpu.VMEM)] * count


def dequantize(words_ref, scales_ref, owned):
    words = words_ref.shape[0]
    groups = words * 4 // G
    head = lax.axis_index("head")
    quant = lax.axis_index("quant")
    scale = scales_ref[
        pl.ds(pl.multiple_of(head * groups, groups), groups),
        pl.ds(pl.multiple_of(quant * HD, HD), HD),
    ]
    spread = jnp.broadcast_to(scale[:, None, :], (groups, words // groups, HD)).reshape(
        words, HD
    )
    held = words_ref[...]
    for k in range(4):
        codes = jnp.bitwise_and(jnp.right_shift(held, 4 * k), 15)
        owned[pl.ds(k, words, stride=4), :] = (codes - 8).astype(jnp.float32) * spread


def one_hot(rows, numbers, first=0):
    at = lax.broadcasted_iota(jnp.int32, (rows, numbers.shape[1]), 0) + first
    return jnp.where(at == numbers, 1.0, 0.0).astype(jnp.bfloat16)


def in_lanes(block):
    return jnp.concatenate([block[s : s + 1, :] for s in range(block.shape[0])], axis=1)


def pack_kernel(words_ref, scales_ref, order_ref, packed_ref, owned_ref, most_ref, owned):
    dequantize(words_ref, scales_ref, owned)
    rows = owned.shape[0]
    lines = rows // HD
    parts = packed_ref.shape[0]
    head = lax.axis_index("head")
    block = owned[...].astype(jnp.bfloat16)
    owned_ref[...] = block
    fullest = jnp.float32(0.0)
    for source in range(parts):
        to = order_ref[source * lines : (source + 1) * lines, :] // rows
        for d in range(parts):
            count = jnp.sum(jnp.where(to == d, 1.0, 0.0))
            fullest = jnp.maximum(fullest, count)
    most_ref[0, 0] = fullest.astype(jnp.int32)
    mine = order_ref[pl.ds(pl.multiple_of(head * lines, lines), lines), :]
    goes = mine // rows
    upto = jnp.where(
        lax.broadcasted_iota(jnp.int32, (HD, HD), 0)
        <= lax.broadcasted_iota(jnp.int32, (HD, HD), 1),
        1.0,
        0.0,
    ).astype(jnp.bfloat16)
    feature = mine % rows
    halves = jnp.concatenate(
        [in_lanes(feature // 32), in_lanes(feature % 32)], axis=0
    ).astype(jnp.float32)
    halves = jnp.concatenate([halves] + [jnp.zeros_like(halves)] * 3, axis=0)
    halves = halves.astype(jnp.bfloat16)
    for d in range(parts):
        held = jnp.where(goes == d, 1.0, 0.0)
        within = jnp.dot(held.astype(jnp.bfloat16), upto, preferred_element_type=jnp.float32)
        before = jnp.zeros((1, 1), jnp.float32)
        ranks = []
        for s in range(lines):
            ranks.append(within[s : s + 1, :] + before)
            before = before + within[s : s + 1, HD - 1 : HD]
        rank = jnp.concatenate(ranks, axis=0)
        rank = jnp.where(goes == d, rank - 1.0, -1.0).astype(jnp.int32)
        picked = one_hot(CAP, in_lanes(rank))
        packed_ref[d, :CAP, :] = jnp.dot(
            picked, block, preferred_element_type=jnp.float32
        ).astype(jnp.bfloat16)
        numbers = lax.dot_general(
            halves, picked, (((1,), (1,)), ((), ())), preferred_element_type=jnp.float32
        )
        wide = jnp.concatenate([numbers, jnp.zeros((8, 2 * HD - CAP), jnp.float32)], axis=1)
        packed_ref[d, CAP:, :] = jnp.concatenate([wide[:, :HD], wide[:, HD:]], axis=0).astype(
            jnp.bfloat16
        )


def packed_rows(words, scales, order, parts):
    rows = words.shape[0] * 4
    return pl.pallas_call(
        pack_kernel,
        out_shape=[
            jax.ShapeDtypeStruct((parts, CAP + 16, HD), jnp.bfloat16),
            jax.ShapeDtypeStruct((rows, HD), jnp.bfloat16),
            jax.ShapeDtypeStruct((1, 1), jnp.int32),
        ],
        in_specs=vmem(3),
        out_specs=vmem(2) + [pl.BlockSpec(memory_space=pltpu.SMEM)],
        scratch_shapes=[pltpu.VMEM((rows, HD), jnp.float32)],
        name="pack",
        cost_estimate=cost(1_000_000_000, 3_000_000),
    )(words, scales, order)


def halved(total, outs):
    near, far = total[: total.shape[0] // 2, :], total[total.shape[0] // 2 :, :]
    middle = HD // 2
    for side, ref in enumerate(outs):
        span = slice(side * middle, (side + 1) * middle)
        half = jnp.concatenate([near[:, span], far[:, span]], axis=1).astype(jnp.bfloat16)
        for copy in range(ref.shape[0]):
            ref[copy] = half


def unpack_kernel(packed_ref, low_ref, high_ref):
    rows = low_ref.shape[1] * 2
    total = None
    for source in range(packed_ref.shape[0]):
        tail = packed_ref[source, CAP:, :].astype(jnp.float32).astype(jnp.int32)
        number = jnp.concatenate(
            [tail[0:1, :] * 32 + tail[1:2, :], tail[8:9, :] * 32 + tail[9:10, :]], axis=1
        )
        part = jnp.dot(
            one_hot(rows, number[:, :CAP]),
            packed_ref[source, :CAP, :],
            preferred_element_type=jnp.float32,
        )
        total = part if total is None else total + part
    halved(total, (low_ref, high_ref))


def pick_kernel(order_ref, every_ref, low_ref, high_ref):
    rows = low_ref.shape[1] * 2
    lines = rows // HD
    head = lax.axis_index("head")
    total = None
    for source in range(every_ref.shape[0]):
        order = in_lanes(order_ref[source * lines : (source + 1) * lines, :])
        part = jnp.dot(
            one_hot(rows, order, head * rows),
            every_ref[source],
            preferred_element_type=jnp.float32,
        )
        total = part if total is None else total + part
    halved(total, (low_ref, high_ref))


def row_halves(kernel, rows, *operands):
    return pl.pallas_call(
        kernel,
        out_shape=[jax.ShapeDtypeStruct((8, rows // 2, HD), jnp.bfloat16)] * 2,
        in_specs=vmem(len(operands)),
        out_specs=vmem(2),
        cost_estimate=cost(1_000_000_000, 3_000_000),
    )(*operands)


def exchanged(blocks, axis, groups=None):
    return lax.all_to_all(blocks, axis, 0, 0, axis_index_groups=groups, tiled=True)


def slot_weight(map_ref, own_ref, mate_ref, relative, dz):
    head = lax.axis_index("head")
    served = map_ref[jnp.bitwise_xor(head // 4, relative) * 4 + (head % 4 + dz) % 4]
    same = served % 2 == lax.axis_index("quant") % 2
    kinds = []
    for kind in range(2):
        chip = kind * 4 + served // 2
        kinds.append(jnp.where(same, own_ref[chip], mate_ref[chip]))
    middle = HD // 2
    return jnp.concatenate(
        [
            jnp.concatenate([block[:, :middle] for block in kinds], axis=1),
            jnp.concatenate([block[:, middle:] for block in kinds], axis=1),
        ],
        axis=0,
    )


def products_kernel(plan, map_ref, x_ref, own_ref, mate_ref, *refs):
    outs, weight = refs[: len(plan)], refs[-1]
    listed = [(slot, outs[at], part) for at, slots in enumerate(plan) for part, slot in enumerate(slots)]

    @pl.when(pl.program_id(0) == 0)
    def _():
        for at, (slot, _, _) in enumerate(listed):
            weight[:, at * HD : (at + 1) * HD] = slot_weight(map_ref, own_ref, mate_ref, *slot)

    for first in range(0, len(listed), 2):
        two = listed[first : first + 2]
        got = jnp.dot(
            x_ref[...],
            weight[:, first * HD : (first + len(two)) * HD],
            preferred_element_type=jnp.float32,
        ).astype(jnp.bfloat16)
        for side, (_, ref, part) in enumerate(two):
            ref[part] = got[:, side * HD : (side + 1) * HD]


def products(tokens, head_map, own, mate, start, rows, plan):
    depth = tokens.shape[1]
    slots = sum(len(entry) for entry in plan)
    whole = pl.BlockSpec(memory_space=pltpu.VMEM)
    return pl.pallas_call(
        functools.partial(products_kernel, plan),
        grid=(rows // TILE,),
        out_shape=[jax.ShapeDtypeStruct((len(entry), rows, HD), jnp.bfloat16) for entry in plan],
        in_specs=[
            pl.BlockSpec(memory_space=pltpu.SMEM),
            pl.BlockSpec((TILE, depth), lambda i: (start // TILE + i, 0)),
            whole,
            whole,
        ],
        out_specs=[pl.BlockSpec((len(entry), TILE, HD), lambda i: (0, i, 0)) for entry in plan],
        scratch_shapes=[pltpu.VMEM((depth, slots * HD), jnp.bfloat16)],
        cost_estimate=cost(2 * depth * HD * slots * rows, 6_000_000),
    )(head_map, tokens, own, mate)


def added(*terms):
    total = terms[0].astype(jnp.float32)
    for term in terms[1:]:
        total = total + term.astype(jnp.float32)
    return total.astype(jnp.bfloat16)


def body(tokens, packed_words, scales, act_order, head_map):
    rows, depth = tokens.shape
    heads = lax.axis_size("head")
    order = act_order.reshape(-1, HD)
    packed, owned, most = packed_rows(packed_words, scales, order, heads)

    def few(packed, owned):
        return tuple(row_halves(unpack_kernel, depth, exchanged(packed, "head")))

    def many(packed, owned):
        every = exchanged(jnp.broadcast_to(owned[None], (heads, *owned.shape)), "head")
        return tuple(row_halves(pick_kernel, depth, order, every))

    low, high = lax.cond(most[0, 0] <= CAP, few, many, packed, owned)
    chips = [[y * 4 + x * 2 + c for y in range(4) for x in range(2)] for c in range(2)]
    low_own = exchanged(low, "quant", chips)
    high_own = exchanged(high, "quant", chips)
    low_mate = over_quant(low_own, 0, 0, 1)
    high_mate = over_quant(high_own, 0, 0, 1)

    relay_up, relay_down = products(
        tokens, head_map, low_own, low_mate, 0, rows, [[(0, 2)], [(1, 2)]]
    )
    relay_up = over_head(relay_up, 0, 1)
    relay_down = over_head(relay_down, 0, -1)
    direct_up, direct_down, turn_up, turn_down, keep, send = products(
        tokens, head_map, low_own, low_mate, 0, rows,
        [[slot] for slot in ((1, 1), (0, 3), (0, 1), (1, 3), (0, 0), (1, 0))],
    )
    direct_up = over_head(direct_up, 0, 1)
    direct_down = over_head(direct_down, 0, -1)
    turn_up = over_head(added(turn_up, relay_up), 0, 1)
    turn_down = over_head(added(turn_down, relay_down), 0, -1)
    across = over_head(added(send, direct_up, turn_down), 1, 0)
    low_sum = added(keep, turn_up, direct_down, across)[0]

    half = rows // 2
    (cross,) = products(
        tokens, head_map, high_own, high_mate, 0, half, [[(1, dz) for dz in range(4)]]
    )
    cross = over_head(cross, 1, 0)
    up, down, far, near = products(
        tokens, head_map, high_own, high_mate, half, half,
        [[(0, dz), (1, dz)] for dz in (1, 3, 2, 0)],
    )
    up = over_head(up, 0, 1)
    down = over_head(down, 0, -1)
    far = over_head(far, 0, 2)
    (stay,) = products(
        tokens, head_map, high_own, high_mate, 0, half, [[(0, dz) for dz in range(4)]]
    )
    joined = [added(stay[dz], cross[dz]) for dz in range(4)]
    first_up = over_head(joined[1], 0, 1)
    first_down = over_head(joined[3], 0, -1)
    first_far = over_head(joined[2], 0, 2)
    across = over_head(added(near[1], up[1], down[1], far[1]), 1, 0)
    high_first = added(joined[0], first_up, first_down, first_far)
    high_second = added(near[0], up[0], down[0], far[0], across)
    high_sum = jnp.concatenate([high_first, high_second], axis=0)
    middle = HD // 2
    keys_out = jnp.concatenate([low_sum[:, :middle], high_sum[:, :middle]], axis=1)
    values_out = jnp.concatenate([low_sum[:, middle:], high_sum[:, middle:]], axis=1)
    return keys_out, values_out


def solution(mesh):
    placed = (P("quant", "head"), P("head", "quant"), P(), P(), P())
    return jax.shard_map(
        body,
        mesh=mesh,
        in_specs=placed,
        out_specs=(P("quant", "head"), P("quant", "head")),
        check_vma=False,
    )
```

profile of v0, /device:TPU:0, one launch (start us, length us, event | category | flops | bytes accessed | tf_op | source)
XLA Modules:
  0.0 148.9 jit_solution(2876154338284539906)
XLA Ops:
  0.6 4.2 %pack.1 = (bf16[8,208,128]{2,1,0:T(8,128)(2,1)S(1)}, bf16[1024,128]{1,0:T(8,128)(2,1)S(1)}, s32[1,1]{1,0:T(1,128)}) custom-call(s32[256,128]{1,0:T(8,128)} %words_ref.1, f32[64,2048]{1,0:T(8,128)} %scales_ref.1, s32[64,128]{1,0:T(8,128)} %bitcast.21), custom_call_target="tpu_custom_call" | custom-call | flops 1000000000 | bytes 3000000 | tf_op jit(solution)/shard_map/pack/pallas_call | solution.py:122
  5.5 21.7 %conditional.1 = ((bf16[8,512,128]{2,1,0:T(8,128)(2,1)}, bf16[8,512,128]{2,1,0:T(8,128)(2,1)S(1)})) conditional(s32[]{:T(128)} %bitcast.1, (bf16[1024,128]{1,0:T(8,128)(2,1)S(1)}, s32[64,128]{1,0:T(8,128)S(1)}) %tuple.24, bf16[8,208,128]{2,1,0:T(8,128)(2,1)S(1)} %get-tuple-element.28), branch_computations={%region_0.0_spmd, %region_1.0_spmd} | conditional | flops 1000000000 | bytes 9553608 | solution.py:272
  5.6 18.3 %all_to_all.19.packed_ref = bf16[8,208,128]{2,1,0:T(8,128)(2,1)} all-to-all(bf16[8,208,128]{2,1,0:T(8,128)(2,1)S(1)} %param.1), channel_id=1, replica_groups=mesh['quant'=16,'head'=8] {'head'}, dimensions={0} | all-to-all | bytes 851968 | tf_op jit(solution)/shard_map/cond/branch_1_fun/all_to_all | solution.py:191
  23.9 3.3 %branch_1_fun.1 = (bf16[8,512,128]{2,1,0:T(8,128)(2,1)}, bf16[8,512,128]{2,1,0:T(8,128)(2,1)S(1)}) custom-call(bf16[8,208,128]{2,1,0:T(8,128)(2,1)} %all_to_all.19.packed_ref), custom_call_target="tpu_custom_call" | custom-call | flops 1000000000 | bytes 3000000 | tf_op jit(solution)/shard_map/cond/branch_1_fun/pallas_call | solution.py:181
  27.2 18.5 %all_to_all.20.own_ref = bf16[8,512,128]{2,1,0:T(8,128)(2,1)S(1)} all-to-all(bf16[8,512,128]{2,1,0:T(8,128)(2,1)S(1)} %get-tuple-element.38), channel_id=1, replica_groups={{0,16,32,48,64,80,96,112},{8,24,40,56,72,88,104,120},{1,17,33,49,65,81,..., dimensions={0} | all-to-all | bytes 2097152 | tf_op jit(solution)/shard_map/all_to_all | solution.py:191
  45.7 3.6 %all-to-all-start.2 = ((bf16[8,512,128]{2,1,0:T(8,128)(2,1)}), bf16[8,512,128]{2,1,0:T(8,128)(2,1)S(1)}, u32[]{:S(2)}, u32[]{:S(2)}) async-start(bf16[8,512,128]{2,1,0:T(8,128)(2,1)} %get-tuple-element.29), calls=%async_computation.2 | async-start | bytes 2097152 | tf_op jit(solution)/shard_map/all_to_all | solution.py:191
  49.4 13.2 %all-to-all-done.2.own_ref = bf16[8,512,128]{2,1,0:T(8,128)(2,1)S(1)} async-done(((bf16[8,512,128]{2,1,0:T(8,128)(2,1)}), bf16[8,512,128]{2,1,0:T(8,128)(2,1)S(1)}, u32[]{:S(2)}, u32[]{:S(2)}) %all-to-all-start.2) | async-done | bytes 1048608 | tf_op jit(solution)/shard_map/all_to_all | solution.py:191
  62.6 1.0 copy-done.2
  63.6 6.0 %shard_map.72 = (bf16[2,768,128]{2,1,0:T(8,128)(2,1)}, bf16[2,768,128]{2,1,0:T(8,128)(2,1)}, bf16[2,768,128]{2,1,0:T(8,128)(2,1)}, bf16[2,768,128]{2,1,0:T(8,128)(2,1)}) custom-call(s32[8]{0:T(128)} %map_ref.9, bf16[1536,1024]{1,0:T(8,128)(2,1)} %x_ref.9, bf16[8,512,128]{2,1,0:T(8,128)(2,1)} %copy-done, bf16[8,512,128]{2,1,0:T(8,128)(2,1)} %copy-done.2), custom_call_target="tpu_custom_call" | custom-call | flops 1610612736 | bytes 6000000 | tf_op jit(solution)/shard_map/pallas_call | solution.py:236
  69.6 1.5 collective-permute-start.15
  71.0 1.7 %collective-permute-start.14 = (bf16[2,768,128]{2,1,0:T(8,128)(2,1)}, bf16[2,768,128]{2,1,0:T(8,128)(2,1)S(1)}, u32[]{:S(2)}, u32[]{:S(2)}) collective-permute-start(bf16[2,768,128]{2,1,0:T(8,128)(2,1)} %get-tuple-element.41), channel_id=1, source_target_pairs={{0,3},{1,0},{2,1},{3,2},{4,7},{5,4},{6,5},{7,6},{8,11},{9,8},{10,9... | collective-permute-start | bytes 1179656 | tf_op jit(solution)/shard_map/ppermute | solution.py:20
  72.7 0.3 collective-permute-start.13
  73.0 4.9 %shard_map.71 = bf16[4,768,128]{2,1,0:T(8,128)(2,1)} custom-call(s32[8]{0:T(128)} %map_ref.9, bf16[1536,1024]{1,0:T(8,128)(2,1)} %x_ref.9, bf16[8,512,128]{2,1,0:T(8,128)(2,1)} %copy-done, bf16[8,512,128]{2,1,0:T(8,128)(2,1)} %copy-done.2), custom_call_target="tpu_custom_call" | custom-call | flops 805306368 | bytes 6000000 | tf_op jit(solution)/shard_map/pallas_call | solution.py:236
  77.9 2.7 %collective-permute-start.9 = (bf16[4,768,128]{2,1,0:T(8,128)(2,1)}, bf16[4,768,128]{2,1,0:T(8,128)(2,1)S(1)}, u32[]{:S(2)}, u32[]{:S(2)}) collective-permute-start(bf16[4,768,128]{2,1,0:T(8,128)(2,1)} %shard_map.71), channel_id=1, source_target_pairs={{0,4},{1,5},{2,6},{3,7},{4,0},{5,1},{6,2},{7,3},{8,12},{9,13},{10,... | collective-permute-start | bytes 2359304 | tf_op jit(solution)/shard_map/ppermute | solution.py:20
  80.6 6.4 %shard_map.69 = (bf16[1,1536,128]{2,1,0:T(8,128)(2,1)}, bf16[1,1536,128]{2,1,0:T(8,128)(2,1)}) custom-call(s32[8]{0:T(128)} %map_ref.9, bf16[1536,1024]{1,0:T(8,128)(2,1)} %x_ref.9, bf16[8,512,128]{2,1,0:T(8,128)(2,1)} %copy-done.1, bf16[8,512,128]{2,1,0:T(8,128)(2,1)} %collective-permute-done.mate_ref), custom_call_target="tpu_custom_call" | custom-call | flops 805306368 | bytes 6000000 | tf_op jit(solution)/shard_map/pallas_call | solution.py:236
  87.0 3.2 %collective-permute-start.5 = (bf16[1,1536,128]{2,1,0:T(8,128)(2,1)}, bf16[1,1536,128]{2,1,0:T(8,128)(2,1)S(1)}, u32[]{:S(2)}, u32[]{:S(2)}) collective-permute-start(bf16[1,1536,128]{2,1,0:T(8,128)(2,1)} %get-tuple-element.37), channel_id=1, source_target_pairs={{0,3},{1,0},{2,1},{3,2},{4,7},{5,4},{6,5},{7,6},{8,11},{9,8},{10,9... | collective-permute-start | bytes 1179656 | tf_op jit(solution)/shard_map/ppermute | solution.py:20
  90.2 7.7 %shard_map.68 = (bf16[1,1536,128]{2,1,0:T(8,128)(2,1)}, bf16[1,1536,128]{2,1,0:T(8,128)(2,1)}, bf16[1,1536,128]{2,1,0:T(8,128)(2,1)}, bf16[1,1536,128]{2,1,0:T(8...) custom-call(s32[8]{0:T(128)} %map_ref.9, bf16[1536,1024]{1,0:T(8,128)(2,1)} %x_ref.9, ...), custom_call_target="tpu_custom_call" | custom-call | flops 2415919104 | bytes 6000000 | tf_op jit(solution)/shard_map/pallas_call | solution.py:236
  98.0 4.9 %shard_map.70 = bf16[4,768,128]{2,1,0:T(8,128)(2,1)} custom-call(s32[8]{0:T(128)} %map_ref.9, bf16[1536,1024]{1,0:T(8,128)(2,1)} %x_ref.9, bf16[8,512,128]{2,1,0:T(8,128)(2,1)} %copy-done, bf16[8,512,128]{2,1,0:T(8,128)(2,1)} %copy-done.2), custom_call_target="tpu_custom_call" | custom-call | flops 805306368 | bytes 6000000 | tf_op jit(solution)/shard_map/pallas_call | solution.py:236
  103.0 3.2 %collective-permute-start.3 = (bf16[1,1536,128]{2,1,0:T(8,128)(2,1)}, bf16[1,1536,128]{2,1,0:T(8,128)(2,1)S(1)}, u32[]{:S(2)}, u32[]{:S(2)}) collective-permute-start(bf16[1,1536,128]{2,1,0:T(8,128)(2,1)} %get-tuple-element.33), channel_id=1, source_target_pairs={{0,3},{1,0},{2,1},{3,2},{4,7},{5,4},{6,5},{7,6},{8,11},{9,8},{10,9... | collective-permute-start | bytes 1179656 | tf_op jit(solution)/shard_map/ppermute | solution.py:20
  106.3 0.7 collective-permute-start.16
  107.0 1.1 add_convert_fusion.2
  108.1 14.8 %collective-permute-done.1 = bf16[1,1536,128]{2,1,0:T(8,128)(2,1)S(1)} collective-permute-done((bf16[1,1536,128]{2,1,0:T(8,128)(2,1)}, bf16[1,1536,128]{2,1,0:T(8,128)(2,1)S(1)}, u32[]{:S(2)}, u32[]{:S(2)}) %collective-permute-start.1) | collective-permute-done | bytes 393248 | tf_op jit(solution)/shard_map/ppermute | solution.py:20
  123.0 2.1 %collective-permute-start.2 = (bf16[1,1536,128]{2,1,0:T(8,128)(2,1)S(1)}, bf16[1,1536,128]{2,1,0:T(8,128)(2,1)S(1)}, u32[]{:S(2)}, u32[]{:S(2)}) collective-permute-start(bf16[1,1536,128]{2,1,0:T(8,128)(2,1)S(1)} %add_convert_fusion.3), channel_id=1, source_target_pairs={{0,1},{1,2},{2,3},{3,0},{4,5},{5,6},{6,7},{7,4},{8,9},{9,10},{10,1... | collective-permute-start | bytes 1179656 | tf_op jit(solution)/shard_map/ppermute | solution.py:20
  125.5 2.7 %collective-permute-start.11 = (bf16[768,128]{1,0:T(8,128)(2,1)S(1)}, bf16[768,128]{1,0:T(8,128)(2,1)S(1)}, u32[]{:S(2)}, u32[]{:S(2)}) collective-permute-start(bf16[768,128]{1,0:T(8,128)(2,1)S(1)} %get-tuple-element.45), channel_id=1, source_target_pairs={{0,3},{1,0},{2,1},{3,2},{4,7},{5,4},{6,5},{7,6},{8,11},{9,8},{10,9... | collective-permute-start | bytes 589832 | tf_op jit(solution)/shard_map/ppermute | solution.py:20
  128.2 6.7 %collective-permute-done.6 = bf16[1,1536,128]{2,1,0:T(8,128)(2,1)S(1)} collective-permute-done((bf16[1,1536,128]{2,1,0:T(8,128)(2,1)S(1)}, bf16[1,1536,128]{2,1,0:T(8,128)(2,1)S(1)}, u32[]{:S(2)}, u32[]{:S(2)}) %collective-permute-start.6) | collective-permute-done | bytes 393248 | tf_op jit(solution)/shard_map/ppermute | solution.py:20
  134.9 2.9 %collective-permute-start.10 = (bf16[768,128]{1,0:T(8,128)(2,1)S(1)}, bf16[768,128]{1,0:T(8,128)(2,1)S(1)}, u32[]{:S(2)}, u32[]{:S(2)}) collective-permute-start(bf16[768,128]{1,0:T(8,128)(2,1)S(1)} %get-tuple-element.43), channel_id=1, source_target_pairs={{0,1},{1,2},{2,3},{3,0},{4,5},{5,6},{6,7},{7,4},{8,9},{9,10},{10,1... | collective-permute-start | bytes 589832 | tf_op jit(solution)/shard_map/ppermute | solution.py:20
  138.1 0.6 collective-permute-start.7
  138.7 1.8 %collective-permute-done.11 = bf16[768,128]{1,0:T(8,128)(2,1)S(1)} collective-permute-done((bf16[768,128]{1,0:T(8,128)(2,1)S(1)}, bf16[768,128]{1,0:T(8,128)(2,1)S(1)}, u32[]{:S(2)}, u32[]{:S(2)}) %collective-permute-start.11) | collective-permute-done | bytes 196640 | tf_op jit(solution)/shard_map/ppermute | solution.py:20
  140.5 1.4 collective-permute-done.10
  142.1 5.3 %collective-permute-done.7 = bf16[1,1536,128]{2,1,0:T(8,128)(2,1)S(1)} collective-permute-done((bf16[1,1536,128]{2,1,0:T(8,128)(2,1)S(1)}, bf16[1,1536,128]{2,1,0:T(8,128)(2,1)S(1)}, u32[]{:S(2)}, u32[]{:S(2)}) %collective-permute-start.7) | collective-permute-done | bytes 393248 | tf_op jit(solution)/shard_map/ppermute | solution.py:20
  147.4 0.2 fusion.3
  147.8 1.1 fusion.5
  (43 shorter events, 1.5 us)
Async XLA Ops:
  0.6 4.9 %copy-start.8 = (s32[8192]{0:T(1024)S(1)}, s32[8192]{0:T(1024)}, u32[]{:S(2)}) copy-start(s32[8192]{0:T(1024)} %param.10) | copy-start | bytes 98308
  45.7 16.8 %copy-start = (bf16[8,512,128]{2,1,0:T(8,128)(2,1)}, bf16[8,512,128]{2,1,0:T(8,128)(2,1)S(1)}, u32[]{:S(2)}) copy-start(bf16[8,512,128]{2,1,0:T(8,128)(2,1)S(1)} %all_to_all.20.own_ref) | copy-start | bytes 3145732
  45.7 16.8 %all-to-all-start.2 = ((bf16[8,512,128]{2,1,0:T(8,128)(2,1)}), bf16[8,512,128]{2,1,0:T(8,128)(2,1)S(1)}, u32[]{:S(2)}, u32[]{:S(2)}) async-start(bf16[8,512,128]{2,1,0:T(8,128)(2,1)} %get-tuple-element.29), calls=%async_computation.2 | async-start | bytes 2097152 | tf_op jit(solution)/shard_map/all_to_all | solution.py:191
  49.3 13.3 %collective-permute-start.8 = (bf16[8,512,128]{2,1,0:T(8,128)(2,1)S(1)}, bf16[8,512,128]{2,1,0:T(8,128)(2,1)S(1)}, u32[]{:S(2)}, u32[]{:S(2)}) collective-permute-start(bf16[8,512,128]{2,1,0:T(8,128)(2,1)S(1)} %all_to_all.20.own_ref), channel_id=1, source_target_pairs={{0,8},{8,0},{16,24},{24,16},{32,40},{40,32},{48,56},{56,48},{64,72... | collective-permute-start | bytes 3145736 | tf_op jit(solution)/shard_map/ppermute | solution.py:30
  62.6 7.0 %copy-start.1 = (bf16[8,512,128]{2,1,0:T(8,128)(2,1)}, bf16[8,512,128]{2,1,0:T(8,128)(2,1)S(1)}, u32[]{:S(2)}) copy-start(bf16[8,512,128]{2,1,0:T(8,128)(2,1)S(1)} %all-to-all-done.2.own_ref) | copy-start | bytes 3145732
  62.6 18.0 %collective-permute-start = (bf16[8,512,128]{2,1,0:T(8,128)(2,1)S(1)}, bf16[8,512,128]{2,1,0:T(8,128)(2,1)}, u32[]{:S(2)}, u32[]{:S(2)}) collective-permute-start(bf16[8,512,128]{2,1,0:T(8,128)(2,1)S(1)} %all-to-all-done.2.own_ref), channel_id=1, source_target_pairs={{0,8},{8,0},{16,24},{24,16},{32,40},{40,32},{48,56},{56,48},{64,72... | collective-permute-start | bytes 3145736 | tf_op jit(solution)/shard_map/ppermute | solution.py:30
  62.6 1.0 copy-start.2
  69.6 33.3 %collective-permute-start.15 = (bf16[2,768,128]{2,1,0:T(8,128)(2,1)}, bf16[2,768,128]{2,1,0:T(8,128)(2,1)S(1)}, u32[]{:S(2)}, u32[]{:S(2)}) collective-permute-start(bf16[2,768,128]{2,1,0:T(8,128)(2,1)} %get-tuple-element.42), channel_id=1, source_target_pairs={{0,2},{1,3},{2,0},{3,1},{4,6},{5,7},{6,4},{7,5},{8,10},{9,11},{10,... | collective-permute-start | bytes 1179656 | tf_op jit(solution)/shard_map/ppermute | solution.py:20
  71.0 32.0 %collective-permute-start.14 = (bf16[2,768,128]{2,1,0:T(8,128)(2,1)}, bf16[2,768,128]{2,1,0:T(8,128)(2,1)S(1)}, u32[]{:S(2)}, u32[]{:S(2)}) collective-permute-start(bf16[2,768,128]{2,1,0:T(8,128)(2,1)} %get-tuple-element.41), channel_id=1, source_target_pairs={{0,3},{1,0},{2,1},{3,2},{4,7},{5,4},{6,5},{7,6},{8,11},{9,8},{10,9... | collective-permute-start | bytes 1179656 | tf_op jit(solution)/shard_map/ppermute | solution.py:20
  72.7 33.4 %collective-permute-start.13 = (bf16[2,768,128]{2,1,0:T(8,128)(2,1)}, bf16[2,768,128]{2,1,0:T(8,128)(2,1)S(1)}, u32[]{:S(2)}, u32[]{:S(2)}) collective-permute-start(bf16[2,768,128]{2,1,0:T(8,128)(2,1)} %get-tuple-element.40), channel_id=1, source_target_pairs={{0,1},{1,2},{2,3},{3,0},{4,5},{5,6},{6,7},{7,4},{8,9},{9,10},{10,1... | collective-permute-start | bytes 1179656 | tf_op jit(solution)/shard_map/ppermute | solution.py:20
  77.9 47.3 %collective-permute-start.9 = (bf16[4,768,128]{2,1,0:T(8,128)(2,1)}, bf16[4,768,128]{2,1,0:T(8,128)(2,1)S(1)}, u32[]{:S(2)}, u32[]{:S(2)}) collective-permute-start(bf16[4,768,128]{2,1,0:T(8,128)(2,1)} %shard_map.71), channel_id=1, source_target_pairs={{0,4},{1,5},{2,6},{3,7},{4,0},{5,1},{6,2},{7,3},{8,12},{9,13},{10,... | collective-permute-start | bytes 2359304 | tf_op jit(solution)/shard_map/ppermute | solution.py:20
  87.0 19.3 %collective-permute-start.5 = (bf16[1,1536,128]{2,1,0:T(8,128)(2,1)}, bf16[1,1536,128]{2,1,0:T(8,128)(2,1)S(1)}, u32[]{:S(2)}, u32[]{:S(2)}) collective-permute-start(bf16[1,1536,128]{2,1,0:T(8,128)(2,1)} %get-tuple-element.37), channel_id=1, source_target_pairs={{0,3},{1,0},{2,1},{3,2},{4,7},{5,4},{6,5},{7,6},{8,11},{9,8},{10,9... | collective-permute-start | bytes 1179656 | tf_op jit(solution)/shard_map/ppermute | solution.py:20
  97.9 8.2 %copy-start.5 = (bf16[2,768,128]{2,1,0:T(8,128)(2,1)S(1)}, bf16[2,768,128]{2,1,0:T(8,128)(2,1)}, u32[]{:S(2)}) copy-start(bf16[2,768,128]{2,1,0:T(8,128)(2,1)} %get-tuple-element.39) | copy-start | bytes 1179652
  102.9 20.0 %copy-start.6 = (bf16[1,1536,128]{2,1,0:T(8,128)(2,1)S(1)}, bf16[1,1536,128]{2,1,0:T(8,128)(2,1)}, u32[]{:S(2)}) copy-start(bf16[1,1536,128]{2,1,0:T(8,128)(2,1)} %get-tuple-element.31) | copy-start | bytes 1179652
  102.9 22.6 %collective-permute-start.4 = (bf16[1,1536,128]{2,1,0:T(8,128)(2,1)}, bf16[1,1536,128]{2,1,0:T(8,128)(2,1)S(1)}, u32[]{:S(2)}, u32[]{:S(2)}) collective-permute-start(bf16[1,1536,128]{2,1,0:T(8,128)(2,1)} %get-tuple-element.35), channel_id=1, source_target_pairs={{0,1},{1,2},{2,3},{3,0},{4,5},{5,6},{6,7},{7,4},{8,9},{9,10},{10,1... | collective-permute-start | bytes 1179656 | tf_op jit(solution)/shard_map/ppermute | solution.py:20
  103.0 39.1 %collective-permute-start.3 = (bf16[1,1536,128]{2,1,0:T(8,128)(2,1)}, bf16[1,1536,128]{2,1,0:T(8,128)(2,1)S(1)}, u32[]{:S(2)}, u32[]{:S(2)}) collective-permute-start(bf16[1,1536,128]{2,1,0:T(8,128)(2,1)} %get-tuple-element.33), channel_id=1, source_target_pairs={{0,3},{1,0},{2,1},{3,2},{4,7},{5,4},{6,5},{7,6},{8,11},{9,8},{10,9... | collective-permute-start | bytes 1179656 | tf_op jit(solution)/shard_map/ppermute | solution.py:20
  106.2 16.7 %collective-permute-start.1 = (bf16[1,1536,128]{2,1,0:T(8,128)(2,1)}, bf16[1,1536,128]{2,1,0:T(8,128)(2,1)S(1)}, u32[]{:S(2)}, u32[]{:S(2)}) collective-permute-start(bf16[1,1536,128]{2,1,0:T(8,128)(2,1)} %get-tuple-element.32), channel_id=1, source_target_pairs={{0,1},{1,2},{2,3},{3,0},{4,5},{5,6},{6,7},{7,4},{8,9},{9,10},{10,1... | collective-permute-start | bytes 1179656 | tf_op jit(solution)/shard_map/ppermute | solution.py:20
  106.2 19.0 %copy-start.3 = (bf16[4,768,128]{2,1,0:T(8,128)(2,1)S(1)}, bf16[4,768,128]{2,1,0:T(8,128)(2,1)}, u32[]{:S(2)}) copy-start(bf16[4,768,128]{2,1,0:T(8,128)(2,1)} %shard_map.70) | copy-start | bytes 2359300
  106.3 16.7 %collective-permute-start.16 = (bf16[768,128]{1,0:T(8,128)(2,1)S(1)}, bf16[768,128]{1,0:T(8,128)(2,1)S(1)}, u32[]{:S(2)}, u32[]{:S(2)}) collective-permute-start(bf16[768,128]{1,0:T(8,128)(2,1)S(1)} %fusion.14), channel_id=1, source_target_pairs={{0,4},{1,5},{2,6},{3,7},{4,0},{5,1},{6,2},{7,3},{8,12},{9,13},{10,... | collective-permute-start | bytes 589832 | tf_op jit(solution)/shard_map/ppermute | solution.py:20
  108.1 29.7 %copy-start.4 = (bf16[1,1536,128]{2,1,0:T(8,128)(2,1)S(1)}, bf16[1,1536,128]{2,1,0:T(8,128)(2,1)}, u32[]{:S(2)}) copy-start(bf16[1,1536,128]{2,1,0:T(8,128)(2,1)} %get-tuple-element.34) | copy-start | bytes 1179652
  122.9 12.0 %collective-permute-start.6 = (bf16[1,1536,128]{2,1,0:T(8,128)(2,1)S(1)}, bf16[1,1536,128]{2,1,0:T(8,128)(2,1)S(1)}, u32[]{:S(2)}, u32[]{:S(2)}) collective-permute-start(bf16[1,1536,128]{2,1,0:T(8,128)(2,1)S(1)} %add_convert_fusion.2), channel_id=1, source_target_pairs={{0,3},{1,0},{2,1},{3,2},{4,7},{5,4},{6,5},{7,6},{8,11},{9,8},{10,9... | collective-permute-start | bytes 1179656 | tf_op jit(solution)/shard_map/ppermute | solution.py:20
  123.0 19.1 %collective-permute-start.2 = (bf16[1,1536,128]{2,1,0:T(8,128)(2,1)S(1)}, bf16[1,1536,128]{2,1,0:T(8,128)(2,1)S(1)}, u32[]{:S(2)}, u32[]{:S(2)}) collective-permute-start(bf16[1,1536,128]{2,1,0:T(8,128)(2,1)S(1)} %add_convert_fusion.3), channel_id=1, source_target_pairs={{0,1},{1,2},{2,3},{3,0},{4,5},{5,6},{6,7},{7,4},{8,9},{9,10},{10,1... | collective-permute-start | bytes 1179656 | tf_op jit(solution)/shard_map/ppermute | solution.py:20
  125.4 22.0 %copy-start.7 = (bf16[1,1536,128]{2,1,0:T(8,128)(2,1)S(1)}, bf16[1,1536,128]{2,1,0:T(8,128)(2,1)}, u32[]{:S(2)}) copy-start(bf16[1,1536,128]{2,1,0:T(8,128)(2,1)} %get-tuple-element.30) | copy-start | bytes 1179652
  125.4 12.7 %collective-permute-start.12 = (bf16[768,128]{1,0:T(8,128)(2,1)S(1)}, bf16[768,128]{1,0:T(8,128)(2,1)S(1)}, u32[]{:S(2)}, u32[]{:S(2)}) collective-permute-start(bf16[768,128]{1,0:T(8,128)(2,1)S(1)} %get-tuple-element.44), channel_id=1, source_target_pairs={{0,2},{1,3},{2,0},{3,1},{4,6},{5,7},{6,4},{7,5},{8,10},{9,11},{10,... | collective-permute-start | bytes 589832 | tf_op jit(solution)/shard_map/ppermute | solution.py:20
  125.5 15.0 %collective-permute-start.11 = (bf16[768,128]{1,0:T(8,128)(2,1)S(1)}, bf16[768,128]{1,0:T(8,128)(2,1)S(1)}, u32[]{:S(2)}, u32[]{:S(2)}) collective-permute-start(bf16[768,128]{1,0:T(8,128)(2,1)S(1)} %get-tuple-element.45), channel_id=1, source_target_pairs={{0,3},{1,0},{2,1},{3,2},{4,7},{5,4},{6,5},{7,6},{8,11},{9,8},{10,9... | collective-permute-start | bytes 589832 | tf_op jit(solution)/shard_map/ppermute | solution.py:20
  134.9 7.1 %collective-permute-start.10 = (bf16[768,128]{1,0:T(8,128)(2,1)S(1)}, bf16[768,128]{1,0:T(8,128)(2,1)S(1)}, u32[]{:S(2)}, u32[]{:S(2)}) collective-permute-start(bf16[768,128]{1,0:T(8,128)(2,1)S(1)} %get-tuple-element.43), channel_id=1, source_target_pairs={{0,1},{1,2},{2,3},{3,0},{4,5},{5,6},{6,7},{7,4},{8,9},{9,10},{10,1... | collective-permute-start | bytes 589832 | tf_op jit(solution)/shard_map/ppermute | solution.py:20
  138.1 9.3 %collective-permute-start.7 = (bf16[1,1536,128]{2,1,0:T(8,128)(2,1)S(1)}, bf16[1,1536,128]{2,1,0:T(8,128)(2,1)S(1)}, u32[]{:S(2)}, u32[]{:S(2)}) collective-permute-start(bf16[1,1536,128]{2,1,0:T(8,128)(2,1)S(1)} %add_convert_fusion.1), channel_id=1, source_target_pairs={{0,4},{1,5},{2,6},{3,7},{4,0},{5,1},{6,2},{7,3},{8,12},{9,13},{10,... | collective-permute-start | bytes 1179656 | tf_op jit(solution)/shard_map/ppermute | solution.py:20
where the time goes:
time: 150 us; the launch traced here: 149 us
  waiting for transfers between devices  43.3 us (29%)
  Pallas kernels  37.5 us (25%)
  blocking collectives  36.8 us (25%)
  starting transfers between devices  25.3 us (17%)
  other arithmetic  3.24 us (2%)
  between operations  1.52 us (1%)
    all_to_all x2, blocking collectives, exchanged(): lax.all_to_all(blocks, axis, 0, 0, axis_index_groups=groups, tiled=True)  36.8 us
    ppermute x15, waiting for transfers between devices, over_head(): return lax.ppermute(value, 'head', pairs)  30.1 us
    pallas_call x5, Pallas kernels, products(): pl.pallas_call(functools.partial(products_kernel, plan), grid=(rows // TI...  29.9 us
    ppermute x15, starting transfers between devices, over_head(): return lax.ppermute(value, 'head', pairs)  21.7 us
    all_to_all x1, waiting for transfers between devices, exchanged(): lax.all_to_all(blocks, axis, 0, 0, axis_index_groups=groups, tiled=True)  13.2 us
    pallas_call x1, Pallas kernels, packed_rows(): pl.pallas_call(pack_kernel, out_shape=[jax.ShapeDtypeStruct((parts, CAP +...  4.24 us
    all_to_all x1, starting transfers between devices, exchanged(): lax.all_to_all(blocks, axis, 0, 0, axis_index_groups=groups, tiled=True)  3.56 us
    pallas_call x1, Pallas kernels, row_halves(): pl.pallas_call(kernel, out_shape=[jax.ShapeDtypeStruct((8, rows // 2, HD)...  3.34 us
  transfers between devices with their start and end apart: 18, of which 7 were waited for; matrix products, arithmetic and copies ran while one was open for 1% of the time, Pallas kernels for 20%

commit v1 on v0

--- a/solution.py
+++ b/solution.py
@@ -11,6 +11,7 @@
 G = 128
 CAP = 192
 TILE = 256
+ROOMY = pltpu.CompilerParams(vmem_limit_bytes=20 * 1024 * 1024)
 
 
 def over_head(value, dx, dz):
@@ -131,6 +132,7 @@
         scratch_shapes=[pltpu.VMEM((rows, HD), jnp.float32)],
         name="pack",
         cost_estimate=cost(1_000_000_000, 3_000_000),
+        compiler_params=ROOMY,
     )(words, scales, order)
 
 
@@ -184,6 +186,7 @@
         in_specs=vmem(len(operands)),
         out_specs=vmem(2),
         cost_estimate=cost(1_000_000_000, 3_000_000),
+        compiler_params=ROOMY,
     )(*operands)
 
 
@@ -209,43 +212,35 @@
     )
 
 
-def products_kernel(plan, map_ref, x_ref, own_ref, mate_ref, *refs):
+def products_kernel(plan, start, map_ref, x_ref, own_ref, mate_ref, *refs):
     outs, weight = refs[: len(plan)], refs[-1]
     listed = [(slot, outs[at], part) for at, slots in enumerate(plan) for part, slot in enumerate(slots)]
-
-    @pl.when(pl.program_id(0) == 0)
-    def _():
-        for at, (slot, _, _) in enumerate(listed):
-            weight[:, at * HD : (at + 1) * HD] = slot_weight(map_ref, own_ref, mate_ref, *slot)
-
+    rows = outs[0].shape[1]
     for first in range(0, len(listed), 2):
         two = listed[first : first + 2]
-        got = jnp.dot(
-            x_ref[...],
-            weight[:, first * HD : (first + len(two)) * HD],
-            preferred_element_type=jnp.float32,
-        ).astype(jnp.bfloat16)
-        for side, (_, ref, part) in enumerate(two):
-            ref[part] = got[:, side * HD : (side + 1) * HD]
+        for side, (slot, _, _) in enumerate(two):
+            weight[:, side * HD : (side + 1) * HD] = slot_weight(map_ref, own_ref, mate_ref, *slot)
+        for row in range(0, rows, TILE):
+            got = jnp.dot(
+                x_ref[start + row : start + row + TILE, :],
+                weight[...],
+                preferred_element_type=jnp.float32,
+            ).astype(jnp.bfloat16)
+            for side, (_, ref, part) in enumerate(two):
+                ref[part, row : row + TILE, :] = got[:, side * HD : (side + 1) * HD]
 
 
 def products(tokens, head_map, own, mate, start, rows, plan):
     depth = tokens.shape[1]
     slots = sum(len(entry) for entry in plan)
-    whole = pl.BlockSpec(memory_space=pltpu.VMEM)
     return pl.pallas_call(
-        functools.partial(products_kernel, plan),
-        grid=(rows // TILE,),
+        functools.partial(products_kernel, plan, start),
         out_shape=[jax.ShapeDtypeStruct((len(entry), rows, HD), jnp.bfloat16) for entry in plan],
-        in_specs=[
-            pl.BlockSpec(memory_space=pltpu.SMEM),
-            pl.BlockSpec((TILE, depth), lambda i: (start // TILE + i, 0)),
-            whole,
-            whole,
-        ],
-        out_specs=[pl.BlockSpec((len(entry), TILE, HD), lambda i: (0, i, 0)) for entry in plan],
-        scratch_shapes=[pltpu.VMEM((depth, slots * HD), jnp.bfloat16)],
+        in_specs=[pl.BlockSpec(memory_space=pltpu.SMEM)] + vmem(3),
+        out_specs=vmem(len(plan)),
+        scratch_shapes=[pltpu.VMEM((depth, 2 * HD), jnp.bfloat16)],
         cost_estimate=cost(2 * depth * HD * slots * rows, 6_000_000),
+        compiler_params=ROOMY,
     )(head_map, tokens, own, mate)
 
 

time: 150 us -> 137 us (0.913)
  Pallas kernels: 37.5 us -> 21.1 us
  starting transfers between devices: 25.3 us -> 29.8 us
  waiting for transfers between devices: 43.3 us -> 40.8 us
  local copies, waits for them, and re-layouts: 1.2 us -> 3.34 us
    pallas_call x5, Pallas kernels: 29.9 us -> 14.4 us  [products(): pl.pallas_call(functools.partial(products_kernel, plan, start), out_shape...]
    ppermute x15, starting transfers between devices: 21.7 us -> 25.5 us  [over_head(): return lax.ppermute(value, 'head', pairs)]
    ppermute x15, waiting for transfers between devices: 30.1 us -> 27.5 us  [over_head(): return lax.ppermute(value, 'head', pairs)]
    unnamed x18 -> x14, local copies, waits for them, and re-layouts: 1.03 us -> 3.17 us
  transfers between devices with their start and end apart: 18 -> 18, of which waited for: 7 -> 8; matrix products, arithmetic and copies ran while one was open for 1% -> 1% of each run, Pallas kernels for 20% -> 11%
where the time goes in v1:
time: 137 us; the launch traced here: 136 us
  waiting for transfers between devices  40.8 us (30%)
  blocking collectives  37.3 us (27%)
  starting transfers between devices  29.8 us (22%)
  Pallas kernels  21.1 us (15%)
  local copies, waits for them, and re-layouts  3.34 us (2%)
  other arithmetic  2.27 us (2%)
  between operations  1.53 us (1%)
    all_to_all x2, blocking collectives, exchanged(): lax.all_to_all(blocks, axis, 0, 0, axis_index_groups=groups, tiled=True)  37.3 us
    ppermute x15, waiting for transfers between devices, over_head(): return lax.ppermute(value, 'head', pairs)  27.5 us
    ppermute x15, starting transfers between devices, over_head(): return lax.ppermute(value, 'head', pairs)  25.5 us
    pallas_call x5, Pallas kernels, products(): pl.pallas_call(functools.partial(products_kernel, plan, start), out_shape...  14.4 us
    all_to_all x1, waiting for transfers between devices, exchanged(): lax.all_to_all(blocks, axis, 0, 0, axis_index_groups=groups, tiled=True)  13.3 us
    all_to_all x1, starting transfers between devices, exchanged(): lax.all_to_all(blocks, axis, 0, 0, axis_index_groups=groups, tiled=True)  4.23 us
    pallas_call x1, Pallas kernels, packed_rows(): pl.pallas_call(pack_kernel, out_shape=[jax.ShapeDtypeStruct((parts, CAP +...  4 us
    unnamed x14, local copies, waits for them, and re-layouts  3.17 us
  transfers between devices with their start and end apart: 18, of which 8 were waited for; matrix products, arithmetic and copies ran while one was open for 1% of the time, Pallas kernels for 11%

profile of v1, /device:TPU:0, one launch (start us, length us, event | category | flops | bytes accessed | tf_op | source)
XLA Modules:
  0.0 136.1 jit_solution(3818442517205979444)
XLA Ops:
  0.6 1.0 copy-done.4
  1.7 0.9 copy-done.5
  2.6 4.0 %pack.1 = (bf16[8,208,128]{2,1,0:T(8,128)(2,1)S(1)}, bf16[1024,128]{1,0:T(8,128)(2,1)S(1)}, s32[1,1]{1,0:T(1,128)}) custom-call(s32[256,128]{1,0:T(8,128)S(1)} %copy-done.5, f32[64,2048]{1,0:T(8,128)S(1)} %copy-done.4, s32[64,128]{1,0:T(8,128)} %bitcast.21), custom_call_target="tpu_custom_call" | custom-call | flops 1000000000 | bytes 3000000 | tf_op jit(solution)/shard_map/pack/pallas_call | solution.py:123
  7.3 20.9 %conditional.1 = ((bf16[8,512,128]{2,1,0:T(8,128)(2,1)}, bf16[8,512,128]{2,1,0:T(8,128)(2,1)})) conditional(s32[]{:T(128)} %bitcast.1, (bf16[1024,128]{1,0:T(8,128)(2,1)S(1)}, s32[64,128]{1,0:T(8,128)S(1)}) %tuple.24, bf16[8,208,128]{2,1,0:T(8,128)(2,1)S(1)} %get-tuple-element.28), branch_computations={%region_0.0_spmd, %region_1.0_spmd} | conditional | flops 1000000000 | bytes 9553608 | solution.py:267
  7.3 18.2 %all_to_all.19.packed_ref = bf16[8,208,128]{2,1,0:T(8,128)(2,1)S(1)} all-to-all(bf16[8,208,128]{2,1,0:T(8,128)(2,1)S(1)} %param.1), channel_id=1, replica_groups=mesh['quant'=16,'head'=8] {'head'}, dimensions={0} | all-to-all | bytes 851968 | tf_op jit(solution)/shard_map/cond/branch_1_fun/all_to_all | solution.py:194
  25.5 2.7 %branch_1_fun.1 = (bf16[8,512,128]{2,1,0:T(8,128)(2,1)}, bf16[8,512,128]{2,1,0:T(8,128)(2,1)}) custom-call(bf16[8,208,128]{2,1,0:T(8,128)(2,1)S(1)} %all_to_all.19.packed_ref), custom_call_target="tpu_custom_call" | custom-call | flops 1000000000 | bytes 3000000 | tf_op jit(solution)/shard_map/cond/branch_1_fun/pallas_call | solution.py:183
  28.2 19.1 %all_to_all.20.own_ref = bf16[8,512,128]{2,1,0:T(8,128)(2,1)} all-to-all(bf16[8,512,128]{2,1,0:T(8,128)(2,1)} %get-tuple-element.38), channel_id=1, replica_groups={{0,16,32,48,64,80,96,112},{8,24,40,56,72,88,104,120},{1,17,33,49,65,81,..., dimensions={0} | all-to-all | bytes 2097152 | tf_op jit(solution)/shard_map/all_to_all | solution.py:194
  47.3 4.2 %all-to-all-start.2 = ((bf16[8,512,128]{2,1,0:T(8,128)(2,1)}), bf16[8,512,128]{2,1,0:T(8,128)(2,1)}, u32[]{:S(2)}, u32[]{:S(2)}) async-start(bf16[8,512,128]{2,1,0:T(8,128)(2,1)} %get-tuple-element.29), calls=%async_computation.2 | async-start | bytes 2097152 | tf_op jit(solution)/shard_map/all_to_all | solution.py:194
  51.6 13.3 %all-to-all-done.2.own_ref = bf16[8,512,128]{2,1,0:T(8,128)(2,1)} async-done(((bf16[8,512,128]{2,1,0:T(8,128)(2,1)}), bf16[8,512,128]{2,1,0:T(8,128)(2,1)}, u32[]{:S(2)}, u32[]{:S(2)}) %all-to-all-start.2) | async-done | bytes 1048608 | tf_op jit(solution)/shard_map/all_to_all | solution.py:194
  64.9 1.2 copy-done.1
  66.1 3.2 %shard_map.72 = (bf16[2,768,128]{2,1,0:T(8,128)(2,1)S(1)}, bf16[2,768,128]{2,1,0:T(8,128)(2,1)S(1)}, bf16[2,768,128]{2,1,0:T(8,128)(2,1)S(1)}, bf16[2,768,128]{2,1,0:T(8,128)(2,1)S(1)}) custom-call(s32[8]{0:T(128)S(1)} %copy-done.3, bf16[1536,1024]{1,0:T(8,128)(2,1)S(1)} %copy-done, bf16[8,512,128]{2,1,0:T(8,128)(2,1)S(1)} %copy-done.1, ...), custom_call_target="tpu_custom_call" | custom-call | flops 1610612736 | bytes 6000000 | tf_op jit(solution)/shard_map/pallas_call | solution.py:236
  69.4 1.4 %collective-permute-start.15 = (bf16[2,768,128]{2,1,0:T(8,128)(2,1)S(1)}, bf16[2,768,128]{2,1,0:T(8,128)(2,1)S(1)}, u32[]{:S(2)}, u32[]{:S(2)}) collective-permute-start(bf16[2,768,128]{2,1,0:T(8,128)(2,1)S(1)} %get-tuple-element.42), channel_id=1, source_target_pairs={{0,2},{1,3},{2,0},{3,1},{4,6},{5,7},{6,4},{7,5},{8,10},{9,11},{10,... | collective-permute-start | bytes 1179656 | tf_op jit(solution)/shard_map/ppermute | solution.py:21
  70.8 1.7 %collective-permute-start.14 = (bf16[2,768,128]{2,1,0:T(8,128)(2,1)S(1)}, bf16[2,768,128]{2,1,0:T(8,128)(2,1)S(1)}, u32[]{:S(2)}, u32[]{:S(2)}) collective-permute-start(bf16[2,768,128]{2,1,0:T(8,128)(2,1)S(1)} %get-tuple-element.41), channel_id=1, source_target_pairs={{0,3},{1,0},{2,1},{3,2},{4,7},{5,4},{6,5},{7,6},{8,11},{9,8},{10,9... | collective-permute-start | bytes 1179656 | tf_op jit(solution)/shard_map/ppermute | solution.py:21
  72.8 2.4 %shard_map.71 = bf16[4,768,128]{2,1,0:T(8,128)(2,1)S(1)} custom-call(s32[8]{0:T(128)S(1)} %copy-done.3, bf16[1536,1024]{1,0:T(8,128)(2,1)S(1)} %copy-done, bf16[8,512,128]{2,1,0:T(8,128)(2,1)S(1)} %copy-done.1, bf16[8,512,128]{2,1,0:T(8,128)(2,1)} %collective-permute-done.8.mate_ref), custom_call_target="tpu_custom_call" | custom-call | flops 805306368 | bytes 6000000 | tf_op jit(solution)/shard_map/pallas_call | solution.py:236
  75.2 2.9 %collective-permute-start.9 = (bf16[4,768,128]{2,1,0:T(8,128)(2,1)S(1)}, bf16[4,768,128]{2,1,0:T(8,128)(2,1)S(1)}, u32[]{:S(2)}, u32[]{:S(2)}) collective-permute-start(bf16[4,768,128]{2,1,0:T(8,128)(2,1)S(1)} %shard_map.71), channel_id=1, source_target_pairs={{0,4},{1,5},{2,6},{3,7},{4,0},{5,1},{6,2},{7,3},{8,12},{9,13},{10,... | collective-permute-start | bytes 2359304 | tf_op jit(solution)/shard_map/ppermute | solution.py:21
  78.1 2.4 %shard_map.69 = (bf16[1,1536,128]{2,1,0:T(8,128)(2,1)S(1)}, bf16[1,1536,128]{2,1,0:T(8,128)(2,1)S(1)}) custom-call(s32[8]{0:T(128)S(1)} %copy-done.3, bf16[1536,1024]{1,0:T(8,128)(2,1)S(1)} %copy-done, bf16[8,512,128]{2,1,0:T(8,128)(2,1)} %all-to-all-done.2.own_ref, bf16[8,512,128]{2,1,0:T(8,128)(2,1)S(1)} %collective-permute-done.mate_ref), custom_call_target="tpu_custom_call" | custom-call | flops 805306368 | bytes 6000000 | tf_op jit(solution)/shard_map/pallas_call | solution.py:236
  80.5 3.3 %collective-permute-start.5 = (bf16[1,1536,128]{2,1,0:T(8,128)(2,1)S(1)}, bf16[1,1536,128]{2,1,0:T(8,128)(2,1)S(1)}, u32[]{:S(2)}, u32[]{:S(2)}) collective-permute-start(bf16[1,1536,128]{2,1,0:T(8,128)(2,1)S(1)} %get-tuple-element.37), channel_id=1, source_target_pairs={{0,3},{1,0},{2,1},{3,2},{4,7},{5,4},{6,5},{7,6},{8,11},{9,8},{10,9... | collective-permute-start | bytes 1179656 | tf_op jit(solution)/shard_map/ppermute | solution.py:21
  83.8 4.0 %shard_map.68 = (bf16[1,1536,128]{2,1,0:T(8,128)(2,1)S(1)}, bf16[1,1536,128]{2,1,0:T(8,128)(2,1)S(1)}, bf16[1,1536,128]{2,1,0:T(8,128)(2,1)S(1)}, bf16[1,1536,12...) custom-call(s32[8]{0:T(128)S(1)} %copy-done.3, ...), custom_call_target="tpu_custom_call" | custom-call | flops 2415919104 | bytes 6000000 | tf_op jit(solution)/shard_map/pallas_call | solution.py:236
  87.8 2.4 %shard_map.70 = bf16[4,768,128]{2,1,0:T(8,128)(2,1)S(1)} custom-call(s32[8]{0:T(128)S(1)} %copy-done.3, bf16[1536,1024]{1,0:T(8,128)(2,1)S(1)} %copy-done, bf16[8,512,128]{2,1,0:T(8,128)(2,1)S(1)} %copy-done.2, bf16[8,512,128]{2,1,0:T(8,128)(2,1)} %collective-permute-done.8.mate_ref), custom_call_target="tpu_custom_call" | custom-call | flops 805306368 | bytes 6000000 | tf_op jit(solution)/shard_map/pallas_call | solution.py:236
  90.3 3.2 %collective-permute-start.3 = (bf16[1,1536,128]{2,1,0:T(8,128)(2,1)S(1)}, bf16[1,1536,128]{2,1,0:T(8,128)(2,1)S(1)}, u32[]{:S(2)}, u32[]{:S(2)}) collective-permute-start(bf16[1,1536,128]{2,1,0:T(8,128)(2,1)S(1)} %get-tuple-element.33), channel_id=1, source_target_pairs={{0,3},{1,0},{2,1},{3,2},{4,7},{5,4},{6,5},{7,6},{8,11},{9,8},{10,9... | collective-permute-start | bytes 1179656 | tf_op jit(solution)/shard_map/ppermute | solution.py:21
  93.7 4.5 %collective-permute-done.5 = bf16[1,1536,128]{2,1,0:T(8,128)(2,1)S(1)} collective-permute-done((bf16[1,1536,128]{2,1,0:T(8,128)(2,1)S(1)}, bf16[1,1536,128]{2,1,0:T(8,128)(2,1)S(1)}, u32[]{:S(2)}, u32[]{:S(2)}) %collective-permute-start.5) | collective-permute-done | bytes 393248 | tf_op jit(solution)/shard_map/ppermute | solution.py:21
  98.2 2.9 %collective-permute-start.16 = (bf16[768,128]{1,0:T(8,128)(2,1)S(1)}, bf16[768,128]{1,0:T(8,128)(2,1)S(1)}, u32[]{:S(2)}, u32[]{:S(2)}) collective-permute-start(bf16[768,128]{1,0:T(8,128)(2,1)S(1)} %fusion.14), channel_id=1, source_target_pairs={{0,4},{1,5},{2,6},{3,7},{4,0},{5,1},{6,2},{7,3},{8,12},{9,13},{10,... | collective-permute-start | bytes 589832 | tf_op jit(solution)/shard_map/ppermute | solution.py:21
  101.2 8.9 %collective-permute-done.1 = bf16[1,1536,128]{2,1,0:T(8,128)(2,1)S(1)} collective-permute-done((bf16[1,1536,128]{2,1,0:T(8,128)(2,1)S(1)}, bf16[1,1536,128]{2,1,0:T(8,128)(2,1)S(1)}, u32[]{:S(2)}, u32[]{:S(2)}) %collective-permute-start.1) | collective-permute-done | bytes 393248 | tf_op jit(solution)/shard_map/ppermute | solution.py:21
  110.2 2.1 %collective-permute-start.2 = (bf16[1,1536,128]{2,1,0:T(8,128)(2,1)S(1)}, bf16[1,1536,128]{2,1,0:T(8,128)(2,1)S(1)}, u32[]{:S(2)}, u32[]{:S(2)}) collective-permute-start(bf16[1,1536,128]{2,1,0:T(8,128)(2,1)S(1)} %add_convert_fusion.3), channel_id=1, source_target_pairs={{0,1},{1,2},{2,3},{3,0},{4,5},{5,6},{6,7},{7,4},{8,9},{9,10},{10,1... | collective-permute-start | bytes 1179656 | tf_op jit(solution)/shard_map/ppermute | solution.py:21
  112.7 2.7 %collective-permute-start.11 = (bf16[768,128]{1,0:T(8,128)(2,1)S(1)}, bf16[768,128]{1,0:T(8,128)(2,1)S(1)}, u32[]{:S(2)}, u32[]{:S(2)}) collective-permute-start(bf16[768,128]{1,0:T(8,128)(2,1)S(1)} %get-tuple-element.45), channel_id=1, source_target_pairs={{0,3},{1,0},{2,1},{3,2},{4,7},{5,4},{6,5},{7,6},{8,11},{9,8},{10,9... | collective-permute-start | bytes 589832 | tf_op jit(solution)/shard_map/ppermute | solution.py:21
  115.4 6.7 %collective-permute-done.6 = bf16[1,1536,128]{2,1,0:T(8,128)(2,1)S(1)} collective-permute-done((bf16[1,1536,128]{2,1,0:T(8,128)(2,1)S(1)}, bf16[1,1536,128]{2,1,0:T(8,128)(2,1)S(1)}, u32[]{:S(2)}, u32[]{:S(2)}) %collective-permute-start.6) | collective-permute-done | bytes 393248 | tf_op jit(solution)/shard_map/ppermute | solution.py:21
  122.1 2.9 %collective-permute-start.10 = (bf16[768,128]{1,0:T(8,128)(2,1)S(1)}, bf16[768,128]{1,0:T(8,128)(2,1)S(1)}, u32[]{:S(2)}, u32[]{:S(2)}) collective-permute-start(bf16[768,128]{1,0:T(8,128)(2,1)S(1)} %get-tuple-element.43), channel_id=1, source_target_pairs={{0,1},{1,2},{2,3},{3,0},{4,5},{5,6},{6,7},{7,4},{8,9},{9,10},{10,1... | collective-permute-start | bytes 589832 | tf_op jit(solution)/shard_map/ppermute | solution.py:21
  125.4 1.9 %collective-permute-start.7 = (bf16[1,1536,128]{2,1,0:T(8,128)(2,1)S(1)}, bf16[1,1536,128]{2,1,0:T(8,128)(2,1)S(1)}, u32[]{:S(2)}, u32[]{:S(2)}) collective-permute-start(bf16[1,1536,128]{2,1,0:T(8,128)(2,1)S(1)} %add_convert_fusion.1), channel_id=1, source_target_pairs={{0,4},{1,5},{2,6},{3,7},{4,0},{5,1},{6,2},{7,3},{8,12},{9,13},{10,... | collective-permute-start | bytes 1179656 | tf_op jit(solution)/shard_map/ppermute | solution.py:21
  127.2 0.5 collective-permute-done.11
  127.8 1.4 %collective-permute-done.10 = bf16[768,128]{1,0:T(8,128)(2,1)S(1)} collective-permute-done((bf16[768,128]{1,0:T(8,128)(2,1)S(1)}, bf16[768,128]{1,0:T(8,128)(2,1)S(1)}, u32[]{:S(2)}, u32[]{:S(2)}) %collective-permute-start.10) | collective-permute-done | bytes 196640 | tf_op jit(solution)/shard_map/ppermute | solution.py:21
  129.4 5.3 %collective-permute-done.7 = bf16[1,1536,128]{2,1,0:T(8,128)(2,1)S(1)} collective-permute-done((bf16[1,1536,128]{2,1,0:T(8,128)(2,1)S(1)}, bf16[1,1536,128]{2,1,0:T(8,128)(2,1)S(1)}, u32[]{:S(2)}, u32[]{:S(2)}) %collective-permute-start.7) | collective-permute-done | bytes 393248 | tf_op jit(solution)/shard_map/ppermute | solution.py:21
  135.0 1.1 fusion.5
  (39 shorter events, 2.1 us)
Async XLA Ops:
  0.6 1.0 copy-start.4
  1.7 0.9 copy-start.5
  2.6 4.7 %copy-start.6 = (s32[8192]{0:T(1024)S(1)}, s32[8192]{0:T(1024)}, u32[]{:S(2)}) copy-start(s32[8192]{0:T(1024)} %param.10) | copy-start | bytes 98308
  28.2 36.7 %copy-start = (bf16[1536,1024]{1,0:T(8,128)(2,1)S(1)}, bf16[1536,1024]{1,0:T(8,128)(2,1)}, u32[]{:S(2)}) copy-start(bf16[1536,1024]{1,0:T(8,128)(2,1)} %x_ref.9) | copy-start | bytes 9437188
  28.2 36.7 %copy-start.3 = (s32[8]{0:T(128)S(1)}, s32[8]{0:T(128)}, u32[]{:S(2)}) copy-start(s32[8]{0:T(128)} %map_ref.9) | copy-start | bytes 100
  47.3 17.6 %all-to-all-start.2 = ((bf16[8,512,128]{2,1,0:T(8,128)(2,1)}), bf16[8,512,128]{2,1,0:T(8,128)(2,1)}, u32[]{:S(2)}, u32[]{:S(2)}) async-start(bf16[8,512,128]{2,1,0:T(8,128)(2,1)} %get-tuple-element.29), calls=%async_computation.2 | async-start | bytes 2097152 | tf_op jit(solution)/shard_map/all_to_all | solution.py:194
  51.5 13.4 %collective-permute-start.8 = (bf16[8,512,128]{2,1,0:T(8,128)(2,1)}, bf16[8,512,128]{2,1,0:T(8,128)(2,1)}, u32[]{:S(2)}, u32[]{:S(2)}) collective-permute-start(bf16[8,512,128]{2,1,0:T(8,128)(2,1)} %all_to_all.20.own_ref), channel_id=1, source_target_pairs={{0,8},{8,0},{16,24},{24,16},{32,40},{40,32},{48,56},{56,48},{64,72... | collective-permute-start | bytes 3145736 | tf_op jit(solution)/shard_map/ppermute | solution.py:31
  64.9 13.2 %collective-permute-start = (bf16[8,512,128]{2,1,0:T(8,128)(2,1)}, bf16[8,512,128]{2,1,0:T(8,128)(2,1)S(1)}, u32[]{:S(2)}, u32[]{:S(2)}) collective-permute-start(bf16[8,512,128]{2,1,0:T(8,128)(2,1)} %all-to-all-done.2.own_ref), channel_id=1, source_target_pairs={{0,8},{8,0},{16,24},{24,16},{32,40},{40,32},{48,56},{56,48},{64,72... | collective-permute-start | bytes 3145736 | tf_op jit(solution)/shard_map/ppermute | solution.py:31
  64.9 1.2 copy-start.1
  69.4 20.9 %collective-permute-start.15 = (bf16[2,768,128]{2,1,0:T(8,128)(2,1)S(1)}, bf16[2,768,128]{2,1,0:T(8,128)(2,1)S(1)}, u32[]{:S(2)}, u32[]{:S(2)}) collective-permute-start(bf16[2,768,128]{2,1,0:T(8,128)(2,1)S(1)} %get-tuple-element.42), channel_id=1, source_target_pairs={{0,2},{1,3},{2,0},{3,1},{4,6},{5,7},{6,4},{7,5},{8,10},{9,11},{10,... | collective-permute-start | bytes 1179656 | tf_op jit(solution)/shard_map/ppermute | solution.py:21
  70.8 19.5 %collective-permute-start.14 = (bf16[2,768,128]{2,1,0:T(8,128)(2,1)S(1)}, bf16[2,768,128]{2,1,0:T(8,128)(2,1)S(1)}, u32[]{:S(2)}, u32[]{:S(2)}) collective-permute-start(bf16[2,768,128]{2,1,0:T(8,128)(2,1)S(1)} %get-tuple-element.41), channel_id=1, source_target_pairs={{0,3},{1,0},{2,1},{3,2},{4,7},{5,4},{6,5},{7,6},{8,11},{9,8},{10,9... | collective-permute-start | bytes 1179656 | tf_op jit(solution)/shard_map/ppermute | solution.py:21
  72.5 21.0 %collective-permute-start.13 = (bf16[2,768,128]{2,1,0:T(8,128)(2,1)S(1)}, bf16[2,768,128]{2,1,0:T(8,128)(2,1)S(1)}, u32[]{:S(2)}, u32[]{:S(2)}) collective-permute-start(bf16[2,768,128]{2,1,0:T(8,128)(2,1)S(1)} %get-tuple-element.40), channel_id=1, source_target_pairs={{0,1},{1,2},{2,3},{3,0},{4,5},{5,6},{6,7},{7,4},{8,9},{9,10},{10,1... | collective-permute-start | bytes 1179656 | tf_op jit(solution)/shard_map/ppermute | solution.py:21
  75.2 37.2 %collective-permute-start.9 = (bf16[4,768,128]{2,1,0:T(8,128)(2,1)S(1)}, bf16[4,768,128]{2,1,0:T(8,128)(2,1)S(1)}, u32[]{:S(2)}, u32[]{:S(2)}) collective-permute-start(bf16[4,768,128]{2,1,0:T(8,128)(2,1)S(1)} %shard_map.71), channel_id=1, source_target_pairs={{0,4},{1,5},{2,6},{3,7},{4,0},{5,1},{6,2},{7,3},{8,12},{9,13},{10,... | collective-permute-start | bytes 2359304 | tf_op jit(solution)/shard_map/ppermute | solution.py:21
  80.5 7.3 %copy-start.2 = (bf16[8,512,128]{2,1,0:T(8,128)(2,1)S(1)}, bf16[8,512,128]{2,1,0:T(8,128)(2,1)}, u32[]{:S(2)}) copy-start(bf16[8,512,128]{2,1,0:T(8,128)(2,1)} %all_to_all.20.own_ref) | copy-start | bytes 3145732
  80.5 17.7 %collective-permute-start.5 = (bf16[1,1536,128]{2,1,0:T(8,128)(2,1)S(1)}, bf16[1,1536,128]{2,1,0:T(8,128)(2,1)S(1)}, u32[]{:S(2)}, u32[]{:S(2)}) collective-permute-start(bf16[1,1536,128]{2,1,0:T(8,128)(2,1)S(1)} %get-tuple-element.37), channel_id=1, source_target_pairs={{0,3},{1,0},{2,1},{3,2},{4,7},{5,4},{6,5},{7,6},{8,11},{9,8},{10,9... | collective-permute-start | bytes 1179656 | tf_op jit(solution)/shard_map/ppermute | solution.py:21
  90.3 22.5 %collective-permute-start.4 = (bf16[1,1536,128]{2,1,0:T(8,128)(2,1)S(1)}, bf16[1,1536,128]{2,1,0:T(8,128)(2,1)S(1)}, u32[]{:S(2)}, u32[]{:S(2)}) collective-permute-start(bf16[1,1536,128]{2,1,0:T(8,128)(2,1)S(1)} %get-tuple-element.35), channel_id=1, source_target_pairs={{0,1},{1,2},{2,3},{3,0},{4,5},{5,6},{6,7},{7,4},{8,9},{9,10},{10,1... | collective-permute-start | bytes 1179656 | tf_op jit(solution)/shard_map/ppermute | solution.py:21
  90.3 39.0 %collective-permute-start.3 = (bf16[1,1536,128]{2,1,0:T(8,128)(2,1)S(1)}, bf16[1,1536,128]{2,1,0:T(8,128)(2,1)S(1)}, u32[]{:S(2)}, u32[]{:S(2)}) collective-permute-start(bf16[1,1536,128]{2,1,0:T(8,128)(2,1)S(1)} %get-tuple-element.33), channel_id=1, source_target_pairs={{0,3},{1,0},{2,1},{3,2},{4,7},{5,4},{6,5},{7,6},{8,11},{9,8},{10,9... | collective-permute-start | bytes 1179656 | tf_op jit(solution)/shard_map/ppermute | solution.py:21
  93.6 16.5 %collective-permute-start.1 = (bf16[1,1536,128]{2,1,0:T(8,128)(2,1)S(1)}, bf16[1,1536,128]{2,1,0:T(8,128)(2,1)S(1)}, u32[]{:S(2)}, u32[]{:S(2)}) collective-permute-start(bf16[1,1536,128]{2,1,0:T(8,128)(2,1)S(1)} %get-tuple-element.32), channel_id=1, source_target_pairs={{0,1},{1,2},{2,3},{3,0},{4,5},{5,6},{6,7},{7,4},{8,9},{9,10},{10,1... | collective-permute-start | bytes 1179656 | tf_op jit(solution)/shard_map/ppermute | solution.py:21
  98.2 12.0 %collective-permute-start.16 = (bf16[768,128]{1,0:T(8,128)(2,1)S(1)}, bf16[768,128]{1,0:T(8,128)(2,1)S(1)}, u32[]{:S(2)}, u32[]{:S(2)}) collective-permute-start(bf16[768,128]{1,0:T(8,128)(2,1)S(1)} %fusion.14), channel_id=1, source_target_pairs={{0,4},{1,5},{2,6},{3,7},{4,0},{5,1},{6,2},{7,3},{8,12},{9,13},{10,... | collective-permute-start | bytes 589832 | tf_op jit(solution)/shard_map/ppermute | solution.py:21
  110.1 12.0 %collective-permute-start.6 = (bf16[1,1536,128]{2,1,0:T(8,128)(2,1)S(1)}, bf16[1,1536,128]{2,1,0:T(8,128)(2,1)S(1)}, u32[]{:S(2)}, u32[]{:S(2)}) collective-permute-start(bf16[1,1536,128]{2,1,0:T(8,128)(2,1)S(1)} %add_convert_fusion.2), channel_id=1, source_target_pairs={{0,3},{1,0},{2,1},{3,2},{4,7},{5,4},{6,5},{7,6},{8,11},{9,8},{10,9... | collective-permute-start | bytes 1179656 | tf_op jit(solution)/shard_map/ppermute | solution.py:21
  110.2 19.2 %collective-permute-start.2 = (bf16[1,1536,128]{2,1,0:T(8,128)(2,1)S(1)}, bf16[1,1536,128]{2,1,0:T(8,128)(2,1)S(1)}, u32[]{:S(2)}, u32[]{:S(2)}) collective-permute-start(bf16[1,1536,128]{2,1,0:T(8,128)(2,1)S(1)} %add_convert_fusion.3), channel_id=1, source_target_pairs={{0,1},{1,2},{2,3},{3,0},{4,5},{5,6},{6,7},{7,4},{8,9},{9,10},{10,1... | collective-permute-start | bytes 1179656 | tf_op jit(solution)/shard_map/ppermute | solution.py:21
  112.6 12.7 %collective-permute-start.12 = (bf16[768,128]{1,0:T(8,128)(2,1)S(1)}, bf16[768,128]{1,0:T(8,128)(2,1)S(1)}, u32[]{:S(2)}, u32[]{:S(2)}) collective-permute-start(bf16[768,128]{1,0:T(8,128)(2,1)S(1)} %get-tuple-element.44), channel_id=1, source_target_pairs={{0,2},{1,3},{2,0},{3,1},{4,6},{5,7},{6,4},{7,5},{8,10},{9,11},{10,... | collective-permute-start | bytes 589832 | tf_op jit(solution)/shard_map/ppermute | solution.py:21
  112.7 15.0 %collective-permute-start.11 = (bf16[768,128]{1,0:T(8,128)(2,1)S(1)}, bf16[768,128]{1,0:T(8,128)(2,1)S(1)}, u32[]{:S(2)}, u32[]{:S(2)}) collective-permute-start(bf16[768,128]{1,0:T(8,128)(2,1)S(1)} %get-tuple-element.45), channel_id=1, source_target_pairs={{0,3},{1,0},{2,1},{3,2},{4,7},{5,4},{6,5},{7,6},{8,11},{9,8},{10,9... | collective-permute-start | bytes 589832 | tf_op jit(solution)/shard_map/ppermute | solution.py:21
  122.1 7.1 %collective-permute-start.10 = (bf16[768,128]{1,0:T(8,128)(2,1)S(1)}, bf16[768,128]{1,0:T(8,128)(2,1)S(1)}, u32[]{:S(2)}, u32[]{:S(2)}) collective-permute-start(bf16[768,128]{1,0:T(8,128)(2,1)S(1)} %get-tuple-element.43), channel_id=1, source_target_pairs={{0,1},{1,2},{2,3},{3,0},{4,5},{5,6},{6,7},{7,4},{8,9},{9,10},{10,1... | collective-permute-start | bytes 589832 | tf_op jit(solution)/shard_map/ppermute | solution.py:21
  125.4 9.3 %collective-permute-start.7 = (bf16[1,1536,128]{2,1,0:T(8,128)(2,1)S(1)}, bf16[1,1536,128]{2,1,0:T(8,128)(2,1)S(1)}, u32[]{:S(2)}, u32[]{:S(2)}) collective-permute-start(bf16[1,1536,128]{2,1,0:T(8,128)(2,1)S(1)} %add_convert_fusion.1), channel_id=1, source_target_pairs={{0,4},{1,5},{2,6},{3,7},{4,0},{5,1},{6,2},{7,3},{8,12},{9,13},{10,... | collective-permute-start | bytes 1179656 | tf_op jit(solution)/shard_map/ppermute | solution.py:21
